TPU v7x, 32 devices: a whole 2x2x4 slice. The times are simulated.
32 devices in a mesh: cls: 8 (over z, y), row: 4 (over x, core).
Axes of the slice: x: 2, y: 2, z: 4, core: 2. Of those that a mesh axis runs over, the one named last changes fastest.
Arguments:
- embeddings: float32 [1024, 1024], P('row'), may hold values from -6 to 6
- weights: float32 [1024, 81920], P(('cls', 'row')), may hold values from -4 to 4
- labels: int32 [1024], replicated, may hold values from 0 to 81919, as said below
Outputs:
- weight_update: float32 [1024, 81920], P(None, ('cls', 'row'))
- losses: float32 [2, 1024], replicated
Inputs may be any that keep to these rules, and one draw needn't show every extreme that they name: labels take at most 512 distinct values, at most one in each aligned run of 160 classes; rows may share a label.
All inputs are finite; a program needn't handle non-finite values.
Results may differ from a plain program's by a relative error of at most 0.012.
The roundings to bfloat16 on the way count: a program that leaves them out, or rounds other values in their place, can miss the bound.
Values may be sent and summed in bfloat16 or wider, within the bound.
A program may use at most 128 MiB of HBM per device.

v0:
```python
import jax
import jax.numpy as jnp
from jax import lax
from jax.sharding import PartitionSpec as P

STEPS = 2


learn_rate = 2.0


def shards(embeddings, weights, labels):
    peer_count = lax.axis_size(("cls", "row"))
    examples = lax.all_gather(embeddings.astype(jnp.bfloat16), "row", axis=0, tiled=True)
    row_count = examples.shape[0]
    feature_rows = weights.shape[0]
    class_count = weights.shape[1] // peer_count
    model_width = feature_rows * peer_count
    offset = lax.axis_index(("cls", "row")) * class_count
    columns = lax.broadcasted_iota(jnp.int32, (1, class_count), 1) + offset
    label_hit = columns == labels[:, None]
    pieces = weights.reshape(feature_rows, peer_count, class_count // 128, 128)
    block_weights = lax.all_to_all(pieces, ("cls", "row"), split_axis=1, concat_axis=0, tiled=True)[
        :, 0
    ]
    block_width = block_weights.shape[1] * 128
    flat_weights = block_weights.reshape(block_weights.shape[0], block_width)
    block_logits = jnp.dot(
        examples, flat_weights.astype(jnp.bfloat16), preferred_element_type=jnp.float32
    )
    first_logits = block_logits.reshape(row_count, block_weights.shape[1], 128)
    current = block_weights.reshape(model_width, class_count)
    logits = first_logits.reshape(row_count, class_count)
    starting = current
    loss_rows = []
    for step_index in range(STEPS):
        if step_index > 0:
            logits = jnp.dot(
                examples, current.astype(jnp.bfloat16), preferred_element_type=jnp.float32
            )
        local_peak = jnp.max(logits, axis=1)
        local_picked = jnp.sum(jnp.where(label_hit, logits, 0.0), axis=1)
        row_peak = lax.pmax(local_peak, ("cls", "row"))
        row_total, picked = lax.psum(
            (jnp.sum(jnp.exp(logits - row_peak[:, None]), axis=1), local_picked), ("cls", "row")
        )
        log_norm = row_peak + jnp.log(row_total)
        loss_rows.append(log_norm - picked)
        onehot = jnp.where(label_hit, 1.0, 0.0)
        residual = (jnp.exp(logits - log_norm[:, None]) - onehot).astype(jnp.bfloat16)
        gradient = (
            lax.dot_general(
                examples, residual, (((0,), (0,)), ((), ())), preferred_element_type=jnp.float32
            )
            / row_count
        )
        current = current - learn_rate * gradient
    return (current - starting, jnp.stack(loss_rows))


def solution(mesh):
    placed = (P("row", None), P(("cls", "row"), None), P())
    return jax.shard_map(
        shards,
        mesh=mesh,
        in_specs=placed,
        out_specs=(P(None, ("cls", "row")), P()),
        check_vma=False,
    )
```

profile of v0, /device:TPU:0, one launch (start us, length us, event | category | flops | bytes accessed | tf_op | source)
XLA Modules:
  0.0 568.5 jit_solution(8699041707677321800)
XLA Ops:
  7.2 9.4 %reshape.18 = f32[32,32,20,128]{3,2,1,0:T(8,128)} reshape(f32[32,81920]{1,0:T(8,128)} %param.4) | data formatting | bytes 20971520 | tf_op jit(solution)/shard_map/reshape | solution.py:22
  16.6 14.7 %copy.13 = f32[32,32,20,128]{3,0,2,1:T(8,128)} copy(f32[32,32,20,128]{3,2,1,0:T(8,128)} %reshape.18) | data formatting | bytes 20971520 | tf_op jit(solution)/shard_map/reshape | solution.py:22
  31.3 7.4 %all-to-all-start = ((f32[32,32,20,128]{3,0,2,1:T(8,128)}), f32[32,32,20,128]{3,0,2,1:T(8,128)}, u32[]{:S(2)}, u32[]{:S(2)}) async-start(f32[32,32,20,128]{3,0,2,1:T(8,128)} %copy.13), calls=%async_computation | async-start | bytes 20971520 | tf_op jit(solution)/shard_map/all_to_all | solution.py:23
  38.8 0.2 all-gather.2.cloned.1.call-start
  39.0 0.9 convert_element_type.15
  39.9 0.0 all-gather.2.cloned.1.call-update
  39.9 234.8 %all-to-all-done = f32[32,32,20,128]{3,0,2,1:T(8,128)} async-done(((f32[32,32,20,128]{3,0,2,1:T(8,128)}), f32[32,32,20,128]{3,0,2,1:T(8,128)}, u32[]{:S(2)}, u32[]{:S(2)}) %all-to-all-start) | async-done | bytes 10485792 | tf_op jit(solution)/shard_map/all_to_all | solution.py:23
  274.7 17.8 %copy.14 = f32[32,32,1,20,128]{4,3,1,0,2:T(8,128)} copy(f32[32,32,1,20,128]{4,1,3,0,2:T(8,128)} %bitcast.1) | data formatting | bytes 20971520 | tf_op jit(solution)/shard_map/all_to_all | solution.py:23
  292.5 11.4 %copy.21 = f32[128,8,20,128]{3,1,2,0:T(8,128)} copy(f32[128,8,20,128]{3,2,1,0:T(8,128)} %bitcast.41) | data formatting | bytes 20971520
  303.9 11.4 %copy.15 = f32[1024,2560]{0,1:T(8,128)} copy(f32[1024,2560]{1,0:T(8,128)} %bitcast.42) | data formatting | bytes 20971520 | tf_op jit(solution)/shard_map/reshape;squeeze | solution.py:32
  315.3 11.4 %fusion.35 = (f32[1024]{0:T(1024)S(1)}, f32[1024,2560]{1,0:T(8,128)}) fusion(bf16[1024,1024]{1,0:T(8,128)(2,1)} %all-gather.2.cloned.1.call-done, f32[1024,2560]{1,0:T(8,128)} %bitcast.43), kind=kOutput, calls=%fused_computation.45 | convolution fusion | flops 5373950976 | bytes 23072768 | tf_op jit(solution)/shard_map/dot_general | solution.py:28
  326.6 36.8 %pmax.14 = f32[1024]{0:T(1024)S(1)} all-reduce(f32[1024]{0:T(1024)S(1)} %get-tuple-element.17), channel_id=1, replica_groups=mesh['cls'=8,'row'=4] {'cls','row'}, use_global_device_ids=true, to_apply=%region_1.2 | all-reduce | flops 1024 | bytes 8192 | tf_op jit(solution)/shard_map/pmax | solution.py:43
  363.5 0.0 copy-done.1
  363.5 5.7 %fusion.4 = (f32[1024]{0:T(1024)S(1)}, f32[1024]{0:T(1024)S(1)}) fusion(f32[1024,2560]{1,0:T(8,128)} %get-tuple-element.18, s32[2560]{0:T(1024)S(1)} %iota_add_fusion, s32[1024]{0:T(1024)S(1)} %copy-done.1, f32[1024]{0:T(1024)S(1)} %pmax.14), kind=kLoop, calls=%fused_computation.7 | loop fusion | flops 13105152 | bytes 10512384 | tf_op jit(solution)/shard_map/reduce_sum | solution.py:42
  369.2 41.0 %psum.28 = f32[1024]{0:T(1024)S(1)} all-reduce(f32[1024]{0:T(1024)S(1)} %get-tuple-element.9), channel_id=1, replica_groups=mesh['cls'=8,'row'=4] {'cls','row'}, use_global_device_ids=true, to_apply=%region_3.4 | all-reduce | flops 1024 | bytes 8192 | tf_op jit(solution)/shard_map/psum | solution.py:44
  410.2 12.0 %fusion.14 = f32[2560,1024]{1,0:T(8,128)} fusion(bf16[1024,1024]{1,0:T(8,128)(2,1)} %all-gather.2.cloned.1.call-done, f32[1024,2560]{1,0:T(8,128)} %get-tuple-element.18, s32[2560]{0:T(1024)S(1)} %iota_add_fusion, f32[1024]{0:T(1024)S(1)} %log_add_fusion.1, s32[1024]{0:T(1024)S(1)} %copy-done.1), kind=kOutput, calls=%fused_computation.21 | convolution fusion | flops 5381816320 | bytes 23087104 | tf_op jit(solution)/shard_map/dot_general | solution.py:52
  422.3 12.4 %fusion.36 = (f32[1024]{0:T(1024)S(1)}, f32[2560,1024]{1,0:T(8,128)}) fusion(bf16[1024,1024]{1,0:T(8,128)(2,1)S(1)} %copy-done.2, f32[1024,2560]{0,1:T(8,128)S(1)} %bitcast.45, f32[2560,1024]{1,0:T(8,128)} %fusion.14), kind=kOutput, calls=%fused_computation.46 | convolution fusion | flops 5379193856 | bytes 33558528 | tf_op jit(solution)/shard_map/dot_general | solution.py:38
  434.6 39.6 %pmax.15 = f32[1024]{0:T(1024)S(1)} all-reduce(f32[1024]{0:T(1024)S(1)} %get-tuple-element.19), channel_id=1, replica_groups=mesh['cls'=8,'row'=4] {'cls','row'}, use_global_device_ids=true, to_apply=%region_5.6 | all-reduce | flops 1024 | bytes 8192 | tf_op jit(solution)/shard_map/pmax | solution.py:43
  474.3 11.5 %copy.16 = f32[2560,1024]{0,1:T(8,128)} copy(f32[2560,1024]{1,0:T(8,128)} %get-tuple-element.20) | data formatting | bytes 20971520 | tf_op jit(solution)/shard_map/dot_general | solution.py:38
  485.8 5.6 fusion.5
  491.4 40.7 %all-reduce = (f32[1024]{0:T(1024)S(1)}, f32[1024]{0:T(1024)S(1)}, f32[1024]{0:T(1024)S(1)}) all-reduce(f32[1024]{0:T(1024)S(1)} %get-tuple-element.11, f32[1024]{0:T(1024)S(1)} %get-tuple-element.10, f32[1024]{0:T(1024)S(1)} %get-tuple-element.8), channel_id=1, replica_groups=mesh['cls'=8,'row'=4] {'cls','row'}, use_global_device_ids=true, to_apply=%region_7.8 | all-reduce | flops 3072 | bytes 24576 | tf_op jit(solution)/shard_map/psum | solution.py:44
  532.1 17.2 %fusion.6 = f32[1024,2560]{0,1:T(8,128)} fusion(f32[1024,2560]{0,1:T(8,128)} %copy.15, f32[2560,1024]{1,0:T(8,128)} %fusion.14, bf16[1024,1024]{1,0:T(8,128)(2,1)} %all-gather.2.cloned.1.call-done, f32[2560,1024]{0,1:T(8,128)} %copy.16, f32[1024]{0:T(1024)S(1)} %get-tuple-element.16, s32[2560]{0:T(1024)S(1)} %iota_add_fusion, s32[1024]{0:T(1024)S(1)} %copy-done.1), kind=kOutput, calls=%fused_computation.11 | convolution fusion | flops 5394923520 | bytes 44058624 | tf_op jit(solution)/shard_map/dot_general | solution.py:52
  549.2 11.4 %copy.18 = f32[1024,2560]{1,0:T(8,128)} copy(f32[1024,2560]{0,1:T(8,128)} %fusion.6) | data formatting | bytes 20971520
  560.6 0.6 pad_maximum_fusion
  (17 shorter events, 0.0 us)
Async XLA Ops:
  31.3 7.7 %copy-start = (f32[256,1024]{1,0:T(8,128)S(1)}, f32[256,1024]{1,0:T(8,128)}, u32[]{:S(2)}) copy-start(f32[256,1024]{1,0:T(8,128)} %param.3) | copy-start | bytes 3145732
  31.3 243.4 %all-to-all-start = ((f32[32,32,20,128]{3,0,2,1:T(8,128)}), f32[32,32,20,128]{3,0,2,1:T(8,128)}, u32[]{:S(2)}, u32[]{:S(2)}) async-start(f32[32,32,20,128]{3,0,2,1:T(8,128)} %copy.13), calls=%async_computation | async-start | bytes 20971520 | tf_op jit(solution)/shard_map/all_to_all | solution.py:23
  38.8 276.5 %all-gather.2.cloned.1.call-start = ((), (), s32[]{:S(2)}) async-start(), calls=%async_computation.1 | async-start | bytes 2621440 | tf_op jit(solution)/shard_map/all_gather | solution.py:14
  315.3 48.2 %copy-start.1 = (s32[1024]{0:T(1024)S(1)}, s32[1024]{0:T(1024)}, u32[]{:S(2)}) copy-start(s32[1024]{0:T(1024)} %param.5) | copy-start | bytes 12292
  363.5 58.8 %slice-start = ((s8[10485760]{0:T(1024)(128)(4,1)}), s8[2097152]{0:T(1024)(128)(4,1)S(1)}, s32[]{:S(2)}) async-start(s8[10485760]{0:T(1024)(128)(4,1)} %bitcast.44), calls=%async_computation.2 | async-start | bytes 4194304
  410.2 12.0 %slice-start.1 = ((s8[10485760]{0:T(1024)(128)(4,1)}), s8[4194304]{0:T(1024)(128)(4,1)S(1)}, s32[]{:S(2)}) async-start(s8[10485760]{0:T(1024)(128)(4,1)} %bitcast.44), calls=%async_computation.3 | async-start | bytes 8388608
  410.2 12.0 %slice-start.2 = ((s8[10485760]{0:T(1024)(128)(4,1)}), s8[4194304]{0:T(1024)(128)(4,1)S(1)}, s32[]{:S(2)}) async-start(s8[10485760]{0:T(1024)(128)(4,1)} %bitcast.44), calls=%async_computation.4 | async-start | bytes 8388608
  410.2 12.0 %copy-start.2 = (bf16[1024,1024]{1,0:T(8,128)(2,1)S(1)}, bf16[1024,1024]{1,0:T(8,128)(2,1)}, u32[]{:S(2)}) copy-start(bf16[1024,1024]{1,0:T(8,128)(2,1)} %all-gather.2.cloned.1.call-done) | copy-start | bytes 6291460
Sparse Core Ops, SparseCore 0:
  41.1 74.9 all-gather.1
where the time goes:
time: 575 us; the launch traced here: 569 us
  waiting for transfers between devices  235 us (41%)
  blocking collectives  158 us (27%)
  local copies, waits for them, and re-layouts  87.6 us (15%)
  matrix products  52.9 us (9%)
  between operations  14.6 us (3%)
  other arithmetic  12.8 us (2%)
  starting transfers between devices  7.65 us (1%)
    all_to_all x1, waiting for transfers between devices, shards(): lax.all_to_all(pieces, ('cls', 'row'), split_axis=1, concat_axis=0, tiled...  235 us
    psum x2, blocking collectives, shards(): lax.psum((jnp.sum(jnp.exp(logits - row_peak[:, None]), axis=1), local_pic...  81.7 us
    pmax x2, blocking collectives, shards(): row_peak = lax.pmax(local_peak, ('cls', 'row'))  76.5 us
    dot_general x2, matrix products, shards(): lax.dot_general(examples, residual, (((0,), (0,)), ((), ())), preferred_e...  29.2 us
    reshape x2, local copies, waits for them, and re-layouts, shards(): pieces = weights.reshape(feature_rows, peer_count, class_count // 128, 128)  24.2 us
    unnamed x14, local copies, waits for them, and re-layouts  22.8 us
    all_to_all x1, local copies, waits for them, and re-layouts, shards(): lax.all_to_all(pieces, ('cls', 'row'), split_axis=1, concat_axis=0, tiled...  17.8 us
    dot_general x1, matrix products, shards(): jnp.dot(examples, current.astype(jnp.bfloat16), preferred_element_type=jn...  12.4 us
  transfers between devices with their start and end apart: 2, of which 1 were waited for; matrix products, arithmetic and copies ran while one was open for 7% of the time, Pallas kernels for 0%

commit v1 on v0

v1 whole, which is shorter than its diff:
```python
import jax
import jax.numpy as jnp
from jax import lax
from jax.sharding import PartitionSpec as P

STEPS = 2


learn_rate = 2.0


def shards(embeddings, weights, labels):
    peer_count = lax.axis_size(("cls", "row"))
    examples = lax.all_gather(embeddings.astype(jnp.bfloat16), "row", axis=0, tiled=True)
    row_count = examples.shape[0]
    feature_rows = weights.shape[0]
    class_count = weights.shape[1] // peer_count
    offset = lax.axis_index(("cls", "row")) * class_count
    columns = lax.broadcasted_iota(jnp.int32, (1, class_count), 1) + offset
    label_hit = columns == labels[:, None]
    pieces = weights.astype(jnp.bfloat16).reshape(feature_rows, peer_count, class_count)
    block_weights = lax.all_to_all(
        pieces.transpose(1, 0, 2), ("cls", "row"), split_axis=0, concat_axis=0, tiled=True
    )
    flat_weights = block_weights.reshape(peer_count * feature_rows, class_count)
    first_logits = jnp.dot(examples, flat_weights, preferred_element_type=jnp.float32)
    rate = learn_rate / row_count
    gram = lax.dot_general(
        examples, examples, (((1,), (1,)), ((), ())), preferred_element_type=jnp.float32
    ).astype(jnp.bfloat16)
    total = None
    loss_rows = []
    for step_index in range(STEPS):
        logits = first_logits
        if step_index > 0:
            logits = logits - rate * jnp.dot(gram, total, preferred_element_type=jnp.float32)
        local_peak = jnp.max(logits, axis=1)
        local_total = jnp.sum(jnp.exp(logits - local_peak[:, None]), axis=1)
        local_picked = jnp.sum(jnp.where(label_hit, logits, 0.0), axis=1)
        stats = lax.all_gather(
            jnp.stack([local_peak, local_total, local_picked]), ("cls", "row"), axis=0
        )
        row_peak = jnp.max(stats[:, 0], axis=0)
        row_total = jnp.sum(stats[:, 1] * jnp.exp(stats[:, 0] - row_peak[None, :]), axis=0)
        picked = jnp.sum(stats[:, 2], axis=0)
        log_norm = row_peak + jnp.log(row_total)
        loss_rows.append(log_norm - picked)
        onehot = jnp.where(label_hit, 1.0, 0.0)
        residual = jnp.exp(logits - log_norm[:, None]) - onehot
        if total is not None:
            residual = residual + total.astype(jnp.float32)
        total = residual.astype(jnp.bfloat16)
    update = lax.dot_general(
        examples, total, (((0,), (0,)), ((), ())), preferred_element_type=jnp.float32
    )
    return (-rate * update, jnp.stack(loss_rows))


def solution(mesh):
    placed = (P("row", None), P(("cls", "row"), None), P())
    return jax.shard_map(
        shards,
        mesh=mesh,
        in_specs=placed,
        out_specs=(P(None, ("cls", "row")), P()),
        check_vma=False,
    )
```

time: 575 us -> 297 us (0.52)
  waiting for transfers between devices: 235 us -> 116 us
  blocking collectives: 158 us -> 78.9 us
  local copies, waits for them, and re-layouts: 87.6 us -> 22.5 us
  matrix products: 52.9 us -> 40.7 us
    all_to_all x1, waiting for transfers between devices: 235 us -> 58.6 us  [shards(): lax.all_to_all(pieces.transpose(1, 0, 2), ('cls', 'row'), split_axis=0, c...]
    psum x2 -> x0, blocking collectives: 81.7 us -> none  [shards(): lax.psum((jnp.sum(jnp.exp(logits - row_peak[:, None]), axis=1), local_pic...]
    all_gather x0 -> x2, blocking collectives: none -> 78.9 us  [shards(): lax.all_gather(jnp.stack([local_peak, local_total, local_picked]), ('cls'...]
    pmax x2 -> x0, blocking collectives: 76.5 us -> none  [shards(): row_peak = lax.pmax(local_peak, ('cls', 'row'))]
    all_gather x1, waiting for transfers between devices: 0.01 us -> 57.6 us  [shards(): lax.all_gather(embeddings.astype(jnp.bfloat16), 'row', axis=0, tiled=True)]
    reshape x2 -> x0, local copies, waits for them, and re-layouts: 24.2 us -> none  [shards(): pieces = weights.reshape(feature_rows, peer_count, class_count // 128, 128)]
    all_to_all x1 -> x0, local copies, waits for them, and re-layouts: 17.8 us -> none  [shards(): lax.all_to_all(pieces, ('cls', 'row'), split_axis=1, concat_axis=0, tiled...]
    dot_general x4 -> x3, matrix products: 52.9 us -> 40.7 us  [the longest x1 19 us: shards(): jnp.dot(gram, total, preferred_element_type=jnp.float32)]
  transfers between devices with their start and end apart: 2 -> 2, of which waited for: 1 -> 2; matrix products, arithmetic and copies ran while one was open for 7% -> 0% of each run, Pallas kernels for 0% -> 0%
where the time goes in v1:
time: 297 us; the launch traced here: 296 us
  waiting for transfers between devices  116 us (39%)
  blocking collectives  78.9 us (27%)
  matrix products  40.7 us (14%)
  local copies, waits for them, and re-layouts  22.5 us (8%)
  other arithmetic  16.2 us (5%)
  between operations  14.2 us (5%)
  starting transfers between devices  7.48 us (3%)
    all_gather x2, blocking collectives, shards(): lax.all_gather(jnp.stack([local_peak, local_total, local_picked]), ('cls'...  78.9 us
    all_to_all x1, waiting for transfers between devices, shards(): lax.all_to_all(pieces.transpose(1, 0, 2), ('cls', 'row'), split_axis=0, c...  58.6 us
    all_gather x1, waiting for transfers between devices, shards(): lax.all_gather(embeddings.astype(jnp.bfloat16), 'row', axis=0, tiled=True)  57.6 us
    dot_general x1, matrix products, shards(): jnp.dot(gram, total, preferred_element_type=jnp.float32)  19 us
    unnamed x12, local copies, waits for them, and re-layouts  17.2 us
    dot_general x1, matrix products, shards(): lax.dot_general(examples, total, (((0,), (0,)), ((), ())), preferred_elem...  13.4 us
    reduce_sum x2, other arithmetic, shards(): local_total = jnp.sum(jnp.exp(logits - local_peak[:, None]), axis=1)  9.4 us
    dot_general x1, matrix products, shards(): jnp.dot(examples, flat_weights, preferred_element_type=jnp.float32)  8.33 us
  transfers between devices with their start and end apart: 2, of which 2 were waited for; matrix products, arithmetic and copies ran while one was open for 0% of the time, Pallas kernels for 0%

profile of v1, /device:TPU:0, one launch (start us, length us, event | category | flops | bytes accessed | tf_op | source)
XLA Modules:
  0.0 296.2 jit_solution(13645730214445711569)
XLA Ops:
  7.2 4.5 %convert_element_type.19 = bf16[32,81920]{1,0:T(8,128)(2,1)S(1)} convert(f32[32,81920]{1,0:T(8,128)} %param.4) | non-fusion elementwise | flops 2621440 | bytes 15728640 | tf_op jit(solution)/shard_map/convert_element_type | solution.py:21
  11.7 1.6 copy.25
  13.3 0.0 copy-start.2
  13.3 5.2 %copy.15 = bf16[32,32,2560]{2,1,0:T(8,128)(2,1)} copy(bf16[32,32,2560]{2,0,1:T(8,128)(2,1)S(1)} %bitcast.48) | data formatting | bytes 10485760 | tf_op jit(solution)/shard_map/transpose | solution.py:23
  18.5 7.4 %all-to-all-start = ((bf16[32,32,2560]{2,1,0:T(8,128)(2,1)}), bf16[32,32,2560]{2,1,0:T(8,128)(2,1)}, u32[]{:S(2)}, u32[]{:S(2)}) async-start(bf16[32,32,2560]{2,1,0:T(8,128)(2,1)} %copy.15), calls=%async_computation | async-start | bytes 10485760 | tf_op jit(solution)/shard_map/all_to_all | solution.py:22
  26.0 0.0 all-gather.6.cloned.1.call-start
  26.0 0.9 convert_element_type.18
  26.9 0.0 all-gather.6.cloned.1.call-update
  26.9 57.6 %all-gather.6.cloned.1.call-done = bf16[1024,1024]{1,0:T(8,128)(2,1)} async-done(((bf16[256,1024]{1,0:T(8,128)(2,1)}), bf16[1024,1024]{1,0:T(8,128)(2,1)}) %all-gather.6.cloned.1.call-update) | async-done | bytes 2097168 | tf_op jit(solution)/shard_map/all_gather | solution.py:14
  84.5 58.6 %all-to-all-done = bf16[32,32,2560]{2,1,0:T(8,128)(2,1)} async-done(((bf16[32,32,2560]{2,1,0:T(8,128)(2,1)}), bf16[32,32,2560]{2,1,0:T(8,128)(2,1)}, u32[]{:S(2)}, u32[]{:S(2)}) %all-to-all-start) | async-done | bytes 5242912 | tf_op jit(solution)/shard_map/all_to_all | solution.py:22
  143.2 8.3 %fusion.32 = (f32[1024]{0:T(1024)S(1)}, f32[1024,2560]{1,0:T(8,128)S(1)}) fusion(bf16[1024,1024]{1,0:T(8,128)(2,1)} %all-gather.6.cloned.1.call-done, bf16[1024,2560]{1,0:T(8,128)(2,1)} %bitcast.1), kind=kOutput, calls=%fused_computation.47 | convolution fusion | flops 5371329536 | bytes 17829888 | tf_op jit(solution)/shard_map/dot_general | solution.py:26
  151.5 4.2 %copy-done = f32[1024,2560]{1,0:T(8,128)} copy-done((f32[1024,2560]{1,0:T(8,128)}, f32[1024,2560]{1,0:T(8,128)S(1)}, u32[]{:S(2)}) %copy-start) | copy-done | bytes 10485784
  155.7 3.1 %exponential_reduce_fusion.1 = (f32[1024]{0:T(1024)S(1)}, f32[1024]{0:T(1024)S(1)}) fusion(f32[1024,2560]{1,0:T(8,128)S(1)} %get-tuple-element.31, f32[1024]{0:T(1024)S(1)} %get-tuple-element.30, s32[1024]{0:T(1024)S(1)} %copy-done.3, s32[2560]{0:T(1024)S(1)} %iota_add_fusion), kind=kLoop, calls=%fused_computation.13 | loop fusion | flops 13105152 | bytes 10512384 | tf_op jit(solution)/shard_map/reduce_sum | solution.py:38
  158.8 40.6 %all-gather.2 = f32[32,3,1024]{2,1,0:T(4,128)S(1)} all-gather(f32[1,3,1024]{2,1,0:T(4,128)S(1)} %maximum_bitcast_fusion), channel_id=2, replica_groups=mesh['cls'=8,'row'=4] {'cls','row'}, dimensions={0}, use_global_device_ids=true | all-gather | bytes 405504 | tf_op jit(solution)/shard_map/all_gather | solution.py:40
  199.4 0.3 fusion.31
  199.8 0.1 fusion.23
  199.9 19.0 %fusion.33 = (f32[1024]{0:T(1024)S(1)}, f32[1024,2560]{1,0:T(8,128)}) fusion(f32[1024,2560]{1,0:T(8,128)} %copy-done, f32[1024]{0:T(1024)S(1)} %get-tuple-element.19, s32[2560]{0:T(1024)S(1)} %iota_add_fusion, s32[1024]{0:T(1024)S(1)} %copy-done.3, bf16[1024,1024]{1,0:T(8,128)(2,1)S(1)} %copy-done.4), kind=kOutput, calls=%fused_computation.48 | convolution fusion | flops 7538211840 | bytes 23091200 | tf_op jit(solution)/shard_map/dot_general | solution.py:36
  218.8 6.3 %exponential_reduce_fusion = (f32[1024]{0:T(1024)S(1)}, f32[1024]{0:T(1024)S(1)}) fusion(f32[1024,2560]{1,0:T(8,128)} %get-tuple-element.33, f32[1024]{0:T(1024)S(1)} %get-tuple-element.32, s32[1024]{0:T(1024)S(1)} %copy-done.3, s32[2560]{0:T(1024)S(1)} %iota_add_fusion), kind=kLoop, calls=%fused_computation.11 | loop fusion | flops 13105152 | bytes 10512384 | tf_op jit(solution)/shard_map/reduce_sum | solution.py:38
  225.2 38.3 %all-gather.3 = f32[32,3,1024]{2,1,0:T(4,128)S(1)} all-gather(f32[1,3,1024]{2,1,0:T(4,128)S(1)} %maximum_bitcast_fusion.1), channel_id=3, replica_groups=mesh['cls'=8,'row'=4] {'cls','row'}, dimensions={0}, use_global_device_ids=true | all-gather | bytes 405504 | tf_op jit(solution)/shard_map/all_gather | solution.py:40
  263.5 0.3 fusion.30
  263.8 0.1 fusion.19
  263.9 13.4 %multiply_bitcast_fusion = f32[1024,2560]{0,1:T(8,128)} fusion(bf16[1024,1024]{1,0:T(8,128)(2,1)S(1)} %copy-done.4, f32[1024,2560]{1,0:T(8,128)S(1)} %copy-done.1, f32[1024]{0:T(1024)S(1)} %get-tuple-element.21, s32[2560]{0:T(1024)S(1)} %iota_add_fusion, s32[1024]{0:T(1024)S(1)} %copy-done.3, f32[1024,2560]{1,0:T(8,128)} %copy-done, ...), kind=kOutput, calls=%fused_computation.10 | convolution fusion | flops 5397544960 | bytes 33576960 | tf_op jit(solution)/shard_map/dot_general | solution.py:53
  277.3 11.4 %copy.18 = f32[1024,2560]{1,0:T(8,128)} copy(f32[1024,2560]{0,1:T(8,128)} %multiply_bitcast_fusion) | data formatting | bytes 20971520
  288.7 0.6 pad_maximum_fusion
  (13 shorter events, 0.1 us)
Async XLA Ops:
  13.3 12.7 %copy-start.2 = (f32[256,1024]{1,0:T(8,128)S(1)}, f32[256,1024]{1,0:T(8,128)}, u32[]{:S(2)}) copy-start(f32[256,1024]{1,0:T(8,128)} %param.3) | copy-start | bytes 3145732
  18.5 124.6 %all-to-all-start = ((bf16[32,32,2560]{2,1,0:T(8,128)(2,1)}), bf16[32,32,2560]{2,1,0:T(8,128)(2,1)}, u32[]{:S(2)}, u32[]{:S(2)}) async-start(bf16[32,32,2560]{2,1,0:T(8,128)(2,1)} %copy.15), calls=%async_computation | async-start | bytes 10485760 | tf_op jit(solution)/shard_map/all_to_all | solution.py:22
  26.0 58.6 %all-gather.6.cloned.1.call-start = ((), (), s32[]{:S(2)}) async-start(), calls=%async_computation.1 | async-start | bytes 2621440 | tf_op jit(solution)/shard_map/all_gather | solution.py:14
  143.2 12.6 %copy-start.3 = (s32[1024]{0:T(1024)S(1)}, s32[1024]{0:T(1024)}, u32[]{:S(2)}) copy-start(s32[1024]{0:T(1024)} %param.5) | copy-start | bytes 12292
  151.5 4.2 %copy-start = (f32[1024,2560]{1,0:T(8,128)}, f32[1024,2560]{1,0:T(8,128)S(1)}, u32[]{:S(2)}) copy-start(f32[1024,2560]{1,0:T(8,128)S(1)} %get-tuple-element.31) | copy-start | bytes 31457284
  151.5 48.3 %copy-start.4 = (bf16[1024,1024]{1,0:T(8,128)(2,1)S(1)}, bf16[1024,1024]{1,0:T(8,128)(2,1)}, u32[]{:S(2)}) copy-start(bf16[1024,1024]{1,0:T(8,128)(2,1)} %all-gather.6.cloned.1.call-done) | copy-start | bytes 6291460
  218.8 45.1 %copy-start.1 = (f32[1024,2560]{1,0:T(8,128)S(1)}, f32[1024,2560]{1,0:T(8,128)}, u32[]{:S(2)}) copy-start(f32[1024,2560]{1,0:T(8,128)} %get-tuple-element.33) | copy-start | bytes 31457284
Sparse Core Ops, SparseCore 0:
  28.3 56.1 all-gather.5

commit v2 on v1

--- a/solution.py
+++ b/solution.py
@@ -1,6 +1,10 @@
+import functools
+
 import jax
 import jax.numpy as jnp
 from jax import lax
+from jax.experimental import pallas as pl
+from jax.experimental.pallas import tpu as pltpu
 from jax.sharding import PartitionSpec as P
 
 STEPS = 2
@@ -8,8 +12,354 @@
 
 learn_rate = 2.0
 
+MESH = pl.DeviceIdType.MESH
+LANES = 128
+ROW_TILE = 256
+SUB = 32
+
+
+def exchange_kernel(
+    cls_n,
+    row_n,
+    rate,
+    emb_ref,
+    weights_ref,
+    labels_ref,
+    total_ref,
+    turned_ref,
+    losses_ref,
+    stage,
+    outgoing,
+    incoming,
+    logits,
+    gram,
+    examples,
+    emb_bf,
+    peak_lanes,
+    sum_lanes,
+    pick_lanes,
+    norm_lanes,
+    row_send,
+    row_recv,
+    cls_send,
+    cls_recv,
+    load_sem,
+    out_sem,
+    in_sem,
+    emb_out,
+    emb_in,
+    row_out,
+    row_in,
+    cls_out,
+    cls_in,
+):
+    n = cls_n * row_n
+    my_cls, my_row = lax.axis_index("cls"), lax.axis_index("row")
+    me = my_cls * row_n + my_row
+    chunks, rows, width = logits.shape
+    features = outgoing.shape[2]
+    class_count = chunks * width
+    shard_rows = emb_ref.shape[0]
+    tiles = rows // ROW_TILE
+    groups = width // LANES
+    slabs = rows // LANES
+
+    def place(p):
+        return (lax.div(p, row_n), lax.rem(p, row_n))
+
+    def load(chunk, slot):
+        @pl.loop(0, n)
+        def _(p):
+            start = pl.multiple_of(p * class_count + chunk * width, LANES)
+            pltpu.make_async_copy(
+                weights_ref.at[:, pl.ds(start, width)], stage.at[slot, p], load_sem.at[slot]
+            ).start()
+
+    load(0, 0)
+    load(1, 1)
+
+    barrier = pltpu.get_barrier_semaphore()
+
+    @pl.loop(1, n)
+    def _(k):
+        pl.semaphore_signal(
+            barrier, inc=1, device_id=place(lax.rem(me + k, n)), device_id_type=MESH
+        )
+
+    emb_bf[...] = emb_ref[...].astype(jnp.bfloat16)
+    mine = pl.ds(pl.multiple_of(my_row * shard_rows, shard_rows), shard_rows)
+    examples[mine, :] = emb_bf[...]
+    pl.semaphore_wait(barrier, n - 1)
+
+    @pl.loop(0, chunks)
+    def _(c):
+        slot = lax.rem(c, 2)
+        pltpu.make_async_copy(stage.at[slot], stage.at[slot], load_sem.at[slot]).wait()
+        spot = pl.ds(pl.multiple_of(me * features, features), features)
+
+        def send(j):
+            p = lax.rem(me + j + n // 2, n)
+            outgoing[c, p] = stage[slot, p].astype(jnp.bfloat16)
+            pltpu.make_async_remote_copy(
+                src_ref=outgoing.at[c, p],
+                dst_ref=incoming.at[c, spot],
+                send_sem=out_sem.at[c],
+                recv_sem=in_sem.at[c],
+                device_id=place(p),
+                device_id_type=MESH,
+            ).start()
+
+        pl.loop(0, n // 2)(send)
+        incoming[c, spot] = stage[slot, me].astype(jnp.bfloat16)
+        pl.loop(n // 2 + 1, n)(send)
+
+        @pl.when(c == 0)
+        def _():
+            @pl.loop(1, row_n)
+            def _(k):
+                pltpu.make_async_remote_copy(
+                    src_ref=emb_bf,
+                    dst_ref=examples.at[mine],
+                    send_sem=emb_out,
+                    recv_sem=emb_in,
+                    device_id=(my_cls, lax.rem(my_row + k, row_n)),
+                    device_id_type=MESH,
+                ).start()
+
+        @pl.when(c + 2 < chunks)
+        def _():
+            load(c + 2, slot)
+
+    peers = pl.ds(0, (row_n - 1) * shard_rows)
+    pltpu.make_async_copy(examples.at[peers], examples.at[peers], emb_in).wait()
+
+    @pl.loop(0, tiles)
+    def _(i):
+        here = pl.ds(pl.multiple_of(i * ROW_TILE, ROW_TILE), ROW_TILE)
+        gram[here, :] = lax.dot_general(
+            examples[here, :],
+            examples[...],
+            (((1,), (1,)), ((), ())),
+            preferred_element_type=jnp.float32,
+        ).astype(jnp.bfloat16)
+        turned_ref[:, here] = examples[here, :].astype(jnp.float32).T.astype(jnp.bfloat16)
+
+    lane = lax.broadcasted_iota(jnp.int32, (SUB, LANES), 1)
+
+    def reset():
+        peak_lanes[...] = jnp.full_like(peak_lanes, -3.0e38)
+        sum_lanes[...] = jnp.zeros_like(sum_lanes)
+        pick_lanes[...] = jnp.zeros_like(pick_lanes)
+
+    def hits(spot, c):
+        shifted = labels_ref[spot, :] - c * width
+        return [lane + q * LANES == shifted for q in range(groups)]
+
+    def collect(c, i):
+        @pl.loop(0, ROW_TILE // SUB, unroll=2)
+        def _(u):
+            spot = pl.ds(pl.multiple_of(i * ROW_TILE + u * SUB, SUB), SUB)
+            block = logits[c, spot, :]
+            parts = [block[:, q * LANES : (q + 1) * LANES] for q in range(groups)]
+            old = peak_lanes[spot, :]
+            peak = functools.reduce(jnp.maximum, parts, old)
+            total = sum_lanes[spot, :] * jnp.exp(old - peak)
+            picked = pick_lanes[spot, :]
+            for part, hit in zip(parts, hits(spot, c)):
+                total = total + jnp.exp(part - peak)
+                picked = picked + jnp.where(hit, part, 0.0)
+            peak_lanes[spot, :] = peak
+            sum_lanes[spot, :] = total
+            pick_lanes[spot, :] = picked
+
+    def share(t, send_buf, recv_buf, send_sem, recv_sem, count, mine_at, target):
+        recv_buf[t, mine_at] = send_buf[t]
+
+        @pl.loop(1, count)
+        def _(k):
+            pltpu.make_async_remote_copy(
+                src_ref=send_buf.at[t],
+                dst_ref=recv_buf.at[t, mine_at],
+                send_sem=send_sem.at[t],
+                recv_sem=recv_sem.at[t],
+                device_id=target(k),
+                device_id_type=MESH,
+            ).start()
+
+        every = pl.ds(0, count - 1)
+        pltpu.make_async_copy(recv_buf.at[t, every], recv_buf.at[t, every], recv_sem.at[t]).wait()
+        norms = recv_buf[t, :, :slabs, :]
+        top = jnp.max(norms, axis=0)
+        norm = top + jnp.log(jnp.sum(jnp.exp(norms - top[None]), axis=0))
+        picked = jnp.sum(recv_buf[t, :, slabs:, :], axis=0)
+        pltpu.make_async_copy(recv_buf.at[t, every], recv_buf.at[t, every], send_sem.at[t]).wait()
+        return norm, picked
+
+    def settle(t):
+        for i in range(slabs):
+            part = pl.ds(i * LANES, LANES)
+            peaks = peak_lanes[part, :].T
+            top = jnp.max(peaks, axis=0, keepdims=True)
+            total = jnp.sum(sum_lanes[part, :].T * jnp.exp(peaks - top), axis=0, keepdims=True)
+            row_send[t, i : i + 1, :] = top + jnp.log(total)
+            row_send[t, slabs + i : slabs + i + 1, :] = jnp.sum(
+                pick_lanes[part, :].T, axis=0, keepdims=True
+            )
+        norm, picked = share(
+            t, row_send, row_recv, row_out, row_in, row_n, my_row,
+            lambda k: (my_cls, lax.rem(my_row + k, row_n)),
+        )
+        cls_send[t, :slabs, :] = norm
+        cls_send[t, slabs:, :] = picked
+        norm, picked = share(
+            t, cls_send, cls_recv, cls_out, cls_in, cls_n, my_cls,
+            lambda k: (lax.rem(my_cls + k, cls_n), my_row),
+        )
+        losses_ref[t] = norm - picked
+        for i in range(slabs):
+            norm_lanes[pl.ds(i * LANES, LANES), :] = jnp.broadcast_to(
+                norm[i : i + 1, :], (LANES, LANES)
+            ).T
+
+    def residuals(first):
+        @pl.loop(0, chunks)
+        def _(c):
+            @pl.loop(0, rows // SUB, unroll=2)
+            def _(u):
+                spot = pl.ds(pl.multiple_of(u * SUB, SUB), SUB)
+                norm = norm_lanes[spot, :]
+                block = logits[c, spot, :]
+                for q, hit in enumerate(hits(spot, c)):
+                    columns = slice(q * LANES, (q + 1) * LANES)
+                    value = jnp.exp(block[:, columns] - norm) - jnp.where(hit, 1.0, 0.0)
+                    if not first:
+                        value = value + total_ref[c, spot, columns].astype(jnp.float32)
+                    total_ref[c, spot, columns] = value.astype(jnp.bfloat16)
+
+    reset()
+
+    @pl.loop(0, chunks)
+    def _(c):
+        arrived = pl.ds(0, (n - 1) * features)
+        pltpu.make_async_copy(
+            incoming.at[c, arrived], incoming.at[c, arrived], in_sem.at[c]
+        ).wait()
+
+        @pl.loop(0, tiles)
+        def _(i):
+            here = pl.ds(pl.multiple_of(i * ROW_TILE, ROW_TILE), ROW_TILE)
+            logits[c, here, :] = jnp.dot(
+                examples[here, :], incoming[c], preferred_element_type=jnp.float32
+            )
+            collect(c, i)
+
+    settle(0)
+    residuals(True)
+    for t in range(1, STEPS):
+        reset()
+
+        @pl.loop(0, chunks)
+        def _(c):
+            @pl.loop(0, tiles)
+            def _(i):
+                here = pl.ds(pl.multiple_of(i * ROW_TILE, ROW_TILE), ROW_TILE)
+                change = jnp.dot(
+                    gram[here, :], total_ref[c], preferred_element_type=jnp.float32
+                )
+                logits[c, here, :] = logits[c, here, :] - rate * change
+                collect(c, i)
+
+        settle(t)
+        residuals(False)
+
+    pltpu.make_async_copy(examples.at[peers], examples.at[peers], emb_out).wait()
+
+    @pl.loop(0, chunks)
+    def _(c):
+        sent = pl.ds(0, n - 1)
+        pltpu.make_async_copy(outgoing.at[c, sent], outgoing.at[c, sent], out_sem.at[c]).wait()
+
+
+def update_kernel(rate, turned_ref, total_ref, out_ref):
+    out_ref[...] = -rate * jnp.dot(
+        turned_ref[...], total_ref[0], preferred_element_type=jnp.float32
+    )
+
+
+def fused(embeddings, weights, labels):
+    cls_n, row_n = lax.axis_size("cls"), lax.axis_size("row")
+    n = cls_n * row_n
+    shard_rows, model_width = embeddings.shape
+    rows = shard_rows * row_n
+    features = weights.shape[0]
+    class_count = weights.shape[1] // n
+    width = max(w for w in (128, 256, 384, 512) if class_count % w == 0)
+    chunks = class_count // width
+    rate = learn_rate / rows
+    slabs = rows // LANES
+    offset = lax.axis_index(("cls", "row")) * class_count
+    label_lanes = jnp.broadcast_to((labels - offset)[:, None], (rows, LANES))
+    vmem = pl.BlockSpec(memory_space=pltpu.VMEM)
+    dma = pltpu.SemaphoreType.DMA
+    total, turned, losses = pl.pallas_call(
+        functools.partial(exchange_kernel, cls_n, row_n, rate),
+        out_shape=(
+            jax.ShapeDtypeStruct((chunks, rows, width), jnp.bfloat16),
+            jax.ShapeDtypeStruct((model_width, rows), jnp.bfloat16),
+            jax.ShapeDtypeStruct((STEPS, slabs, LANES), jnp.float32),
+        ),
+        in_specs=[vmem, pl.BlockSpec(memory_space=pl.ANY), vmem],
+        out_specs=(vmem, vmem, vmem),
+        scratch_shapes=[
+            pltpu.VMEM((2, n, features, width), jnp.float32),
+            pltpu.VMEM((chunks, n, features, width), jnp.bfloat16),
+            pltpu.VMEM((chunks, n * features, width), jnp.bfloat16),
+            pltpu.VMEM((chunks, rows, width), jnp.float32),
+            pltpu.VMEM((rows, rows), jnp.bfloat16),
+            pltpu.VMEM((rows, model_width), jnp.bfloat16),
+            pltpu.VMEM((shard_rows, model_width), jnp.bfloat16),
+            pltpu.VMEM((rows, LANES), jnp.float32),
+            pltpu.VMEM((rows, LANES), jnp.float32),
+            pltpu.VMEM((rows, LANES), jnp.float32),
+            pltpu.VMEM((rows, LANES), jnp.float32),
+            pltpu.VMEM((STEPS, 2 * slabs, LANES), jnp.float32),
+            pltpu.VMEM((STEPS, row_n, 2 * slabs, LANES), jnp.float32),
+            pltpu.VMEM((STEPS, 2 * slabs, LANES), jnp.float32),
+            pltpu.VMEM((STEPS, cls_n, 2 * slabs, LANES), jnp.float32),
+            dma((2,)),
+            dma((chunks,)),
+            dma((chunks,)),
+            dma,
+            dma,
+            dma((STEPS,)),
+            dma((STEPS,)),
+            dma((STEPS,)),
+            dma((STEPS,)),
+        ],
+        compiler_params=pltpu.CompilerParams(
+            collective_id=0, has_side_effects=True, vmem_limit_bytes=60 * 1024 * 1024
+        ),
+    )(embeddings, weights, label_lanes)
+    tall = model_width // 2
+    update = pl.pallas_call(
+        functools.partial(update_kernel, rate),
+        grid=(chunks, 2),
+        out_shape=jax.ShapeDtypeStruct((model_width, class_count), jnp.float32),
+        in_specs=[
+            pl.BlockSpec((tall, rows), lambda c, i: (i, 0)),
+            pl.BlockSpec((1, rows, width), lambda c, i: (c, 0, 0)),
+        ],
+        out_specs=pl.BlockSpec((tall, width), lambda c, i: (i, c)),
+        compiler_params=pltpu.CompilerParams(
+            dimension_semantics=("arbitrary", "arbitrary"), vmem_limit_bytes=32 * 1024 * 1024
+        ),
+    )(turned, total)
+    return update, losses.reshape(STEPS, rows)
+
 
 def shards(embeddings, weights, labels):
+    if STEPS == 2 and weights.shape[0] % 16 == 0:
+        return fused(embeddings, weights, labels)
     peer_count = lax.axis_size(("cls", "row"))
     examples = lax.all_gather(embeddings.astype(jnp.bfloat16), "row", axis=0, tiled=True)
     row_count = examples.shape[0]

time: 297 us -> 180 us (0.61)
  Pallas kernels: 0 us -> 172 us
  waiting for transfers between devices: 116 us -> 0 us
  blocking collectives: 78.9 us -> 0 us
  matrix products: 40.7 us -> 0 us
  local copies, waits for them, and re-layouts: 22.5 us -> 6.37 us
  other arithmetic: 16.2 us -> 0.69 us
  between operations: 14.2 us -> 0.65 us
  starting transfers between devices: 7.48 us -> 0 us
    pallas_call x0 -> x2, Pallas kernels: none -> 172 us  [the longest x1 163 us: fused(): pl.pallas_call(functools.partial(exchange_kernel, cls_n, row_n, rate), ou...]
    all_gather x2 -> x0, blocking collectives: 78.9 us -> none  [shards(): lax.all_gather(jnp.stack([local_peak, local_total, local_picked]), ('cls'...]
    all_to_all x1 -> x0, waiting for transfers between devices: 58.6 us -> none  [shards(): lax.all_to_all(pieces.transpose(1, 0, 2), ('cls', 'row'), split_axis=0, c...]
    all_gather x1 -> x0, waiting for transfers between devices: 57.6 us -> none  [shards(): lax.all_gather(embeddings.astype(jnp.bfloat16), 'row', axis=0, tiled=True)]
    dot_general x3 -> x0, matrix products: 40.7 us -> none  [the longest x1 19 us: shards(): jnp.dot(gram, total, preferred_element_type=jnp.float32)]
    unnamed x12 -> x5, local copies, waits for them, and re-layouts: 17.2 us -> 5.38 us
    reduce_sum x4 -> x0, other arithmetic: 9.52 us -> none  [the longest x2 9.4 us: shards(): local_total = jnp.sum(jnp.exp(logits - local_peak[:, None]), axis=1)]
    all_to_all x1 -> x0, starting transfers between devices: 7.44 us -> none  [shards(): lax.all_to_all(pieces.transpose(1, 0, 2), ('cls', 'row'), split_axis=0, c...]
  transfers between devices with their start and end apart: 2 -> 0, of which waited for: 2 -> 0; matrix products, arithmetic and copies ran while one was open for 0% -> 0% of each run, Pallas kernels for 0% -> 0%
where the time goes in v2:
time: 180 us
  Pallas kernels  172 us (96%)
  local copies, waits for them, and re-layouts  6.37 us (4%)
    pallas_call x1, Pallas kernels, fused(): pl.pallas_call(functools.partial(exchange_kernel, cls_n, row_n, rate), ou...  163 us
    pallas_call x1, Pallas kernels, fused(): pl.pallas_call(functools.partial(update_kernel, rate), grid=(chunks, 2),...  9.11 us
    unnamed x5, local copies, waits for them, and re-layouts  5.38 us

profile of v2, /device:TPU:0, one launch (start us, length us, event | category | flops | bytes accessed | tf_op | source)
XLA Modules:
  0.0 179.9 jit_solution(7162467832715199296)
XLA Ops:
  0.6 0.7 broadcast_subtract_fusion
  1.3 1.0 broadcast_in_dim.2.labels_ref
  2.3 163.1 %shard_map.50 = (bf16[5,1024,512]{2,1,0:T(8,128)(2,1)}, bf16[1024,1024]{1,0:T(8,128)(2,1)}, f32[2,8,128]{2,1,0:T(8,128)}) custom-call(f32[256,1024]{1,0:T(8,128)} %emb_ref.1, f32[32,81920]{1,0:T(8,128)} %weights_ref.1, s32[1024,128]{1,0:T(8,128)} %broadcast_in_dim.2.labels_ref), custom_call_target="tpu_custom_call" | custom-call | tf_op jit(solution)/shard_map/pallas_call | solution.py:304
  165.4 1.3 copy.7
  166.7 0.0 copy-start
  166.7 2.5 %copy-done = bf16[5,1024,512]{2,1,0:T(8,128)(2,1)S(1)} copy-done((bf16[5,1024,512]{2,1,0:T(8,128)(2,1)S(1)}, bf16[5,1024,512]{2,1,0:T(8,128)(2,1)}, u32[]{:S(2)}) %copy-start) | copy-done | bytes 5242904
  169.2 0.0 copy-start.1
  169.2 1.6 copy-done.1
  170.8 9.1 %shard_map.51 = f32[1024,2560]{1,0:T(8,128)} custom-call(bf16[1024,1024]{1,0:T(8,128)(2,1)S(1)} %copy-done.1, bf16[5,1024,512]{2,1,0:T(8,128)(2,1)S(1)} %copy-done), custom_call_target="tpu_custom_call" | custom-call | tf_op jit(solution)/shard_map/pallas_call | solution.py:344
Async XLA Ops:
  166.7 2.5 %copy-start = (bf16[5,1024,512]{2,1,0:T(8,128)(2,1)S(1)}, bf16[5,1024,512]{2,1,0:T(8,128)(2,1)}, u32[]{:S(2)}) copy-start(bf16[5,1024,512]{2,1,0:T(8,128)(2,1)} %get-tuple-element.6.total_ref) | copy-start | bytes 15728644
  169.2 1.6 copy-start.1

commit v3 on v2

--- a/solution.py
+++ b/solution.py
@@ -31,6 +31,7 @@
     stage,
     outgoing,
     incoming,
+    label_lanes,
     logits,
     gram,
     examples,
@@ -144,7 +145,10 @@
         ).astype(jnp.bfloat16)
         turned_ref[:, here] = examples[here, :].astype(jnp.float32).T.astype(jnp.bfloat16)
 
-    lane = lax.broadcasted_iota(jnp.int32, (SUB, LANES), 1)
+    for i in range(slabs):
+        label_lanes[pl.ds(i * LANES, LANES), :] = (
+            jnp.broadcast_to(labels_ref[i : i + 1, :], (LANES, LANES)).T - me * class_count
+        )
 
     def reset():
         peak_lanes[...] = jnp.full_like(peak_lanes, -3.0e38)
@@ -152,25 +156,22 @@
         pick_lanes[...] = jnp.zeros_like(pick_lanes)
 
     def hits(spot, c):
-        shifted = labels_ref[spot, :] - c * width
+        shifted = label_lanes[spot, :] - c * width
+        lane = lax.broadcasted_iota(jnp.int32, shifted.shape, 1)
         return [lane + q * LANES == shifted for q in range(groups)]
 
-    def collect(c, i):
-        @pl.loop(0, ROW_TILE // SUB, unroll=2)
-        def _(u):
-            spot = pl.ds(pl.multiple_of(i * ROW_TILE + u * SUB, SUB), SUB)
-            block = logits[c, spot, :]
-            parts = [block[:, q * LANES : (q + 1) * LANES] for q in range(groups)]
-            old = peak_lanes[spot, :]
-            peak = functools.reduce(jnp.maximum, parts, old)
-            total = sum_lanes[spot, :] * jnp.exp(old - peak)
-            picked = pick_lanes[spot, :]
-            for part, hit in zip(parts, hits(spot, c)):
-                total = total + jnp.exp(part - peak)
-                picked = picked + jnp.where(hit, part, 0.0)
-            peak_lanes[spot, :] = peak
-            sum_lanes[spot, :] = total
-            pick_lanes[spot, :] = picked
+    def collect(c, spot, block):
+        parts = [block[:, q * LANES : (q + 1) * LANES] for q in range(groups)]
+        old = peak_lanes[spot, :]
+        peak = functools.reduce(jnp.maximum, parts, old)
+        total = sum_lanes[spot, :] * jnp.exp(old - peak)
+        picked = pick_lanes[spot, :]
+        for part, hit in zip(parts, hits(spot, c)):
+            total = total + jnp.exp(part - peak)
+            picked = picked + jnp.where(hit, part, 0.0)
+        peak_lanes[spot, :] = peak
+        sum_lanes[spot, :] = total
+        pick_lanes[spot, :] = picked
 
     def share(t, send_buf, recv_buf, send_sem, recv_sem, count, mine_at, target):
         recv_buf[t, mine_at] = send_buf[t]
@@ -215,26 +216,22 @@
             t, cls_send, cls_recv, cls_out, cls_in, cls_n, my_cls,
             lambda k: (lax.rem(my_cls + k, cls_n), my_row),
         )
-        losses_ref[t] = norm - picked
+        loss = norm - picked
         for i in range(slabs):
+            losses_ref[t : t + 1, i * LANES : (i + 1) * LANES] = loss[i : i + 1, :]
             norm_lanes[pl.ds(i * LANES, LANES), :] = jnp.broadcast_to(
                 norm[i : i + 1, :], (LANES, LANES)
             ).T
 
-    def residuals(first):
-        @pl.loop(0, chunks)
-        def _(c):
-            @pl.loop(0, rows // SUB, unroll=2)
-            def _(u):
-                spot = pl.ds(pl.multiple_of(u * SUB, SUB), SUB)
-                norm = norm_lanes[spot, :]
-                block = logits[c, spot, :]
-                for q, hit in enumerate(hits(spot, c)):
-                    columns = slice(q * LANES, (q + 1) * LANES)
-                    value = jnp.exp(block[:, columns] - norm) - jnp.where(hit, 1.0, 0.0)
-                    if not first:
-                        value = value + total_ref[c, spot, columns].astype(jnp.float32)
-                    total_ref[c, spot, columns] = value.astype(jnp.bfloat16)
+    def residual(c, spot, earlier):
+        norm = norm_lanes[spot, :]
+        block = logits[c, spot, :]
+        for q, hit in enumerate(hits(spot, c)):
+            columns = slice(q * LANES, (q + 1) * LANES)
+            value = jnp.exp(block[:, columns] - norm) - jnp.where(hit, 1.0, 0.0)
+            if earlier:
+                value = value + total_ref[c, spot, columns].astype(jnp.float32)
+            total_ref[c, spot, columns] = value.astype(jnp.bfloat16)
 
     reset()
 
@@ -251,26 +248,36 @@
             logits[c, here, :] = jnp.dot(
                 examples[here, :], incoming[c], preferred_element_type=jnp.float32
             )
-            collect(c, i)
+
+            @pl.loop(0, ROW_TILE // SUB, unroll=2)
+            def _(u):
+                spot = pl.ds(pl.multiple_of(i * ROW_TILE + u * SUB, SUB), SUB)
+                collect(c, spot, logits[c, spot, :])
 
     settle(0)
-    residuals(True)
-    for t in range(1, STEPS):
-        reset()
-
-        @pl.loop(0, chunks)
-        def _(c):
-            @pl.loop(0, tiles)
-            def _(i):
-                here = pl.ds(pl.multiple_of(i * ROW_TILE, ROW_TILE), ROW_TILE)
-                change = jnp.dot(
-                    gram[here, :], total_ref[c], preferred_element_type=jnp.float32
-                )
-                logits[c, here, :] = logits[c, here, :] - rate * change
-                collect(c, i)
-
-        settle(t)
-        residuals(False)
+    reset()
+
+    @pl.loop(0, rows // SUB, unroll=4)
+    def _(u):
+        residual(0, pl.ds(pl.multiple_of(u * SUB, SUB), SUB), False)
+
+    for c in range(chunks):
+        for i in range(tiles):
+            here = pl.ds(i * ROW_TILE, ROW_TILE)
+            change = jnp.dot(gram[here, :], total_ref[c], preferred_element_type=jnp.float32)
+            if c + 1 < chunks:
+                residual(c + 1, here, False)
+            block = logits[c, here, :] - rate * change
+            logits[c, here, :] = block
+            collect(c, here, block)
+
+    settle(1)
+
+    @pl.loop(0, chunks)
+    def _(c):
+        @pl.loop(0, rows // SUB, unroll=4)
+        def _(u):
+            residual(c, pl.ds(pl.multiple_of(u * SUB, SUB), SUB), True)
 
     pltpu.make_async_copy(examples.at[peers], examples.at[peers], emb_out).wait()
 
@@ -297,8 +304,6 @@
     chunks = class_count // width
     rate = learn_rate / rows
     slabs = rows // LANES
-    offset = lax.axis_index(("cls", "row")) * class_count
-    label_lanes = jnp.broadcast_to((labels - offset)[:, None], (rows, LANES))
     vmem = pl.BlockSpec(memory_space=pltpu.VMEM)
     dma = pltpu.SemaphoreType.DMA
     total, turned, losses = pl.pallas_call(
@@ -306,7 +311,7 @@
         out_shape=(
             jax.ShapeDtypeStruct((chunks, rows, width), jnp.bfloat16),
             jax.ShapeDtypeStruct((model_width, rows), jnp.bfloat16),
-            jax.ShapeDtypeStruct((STEPS, slabs, LANES), jnp.float32),
+            jax.ShapeDtypeStruct((STEPS, rows), jnp.float32),
         ),
         in_specs=[vmem, pl.BlockSpec(memory_space=pl.ANY), vmem],
         out_specs=(vmem, vmem, vmem),
@@ -314,6 +319,7 @@
             pltpu.VMEM((2, n, features, width), jnp.float32),
             pltpu.VMEM((chunks, n, features, width), jnp.bfloat16),
             pltpu.VMEM((chunks, n * features, width), jnp.bfloat16),
+            pltpu.VMEM((rows, LANES), jnp.int32),
             pltpu.VMEM((chunks, rows, width), jnp.float32),
             pltpu.VMEM((rows, rows), jnp.bfloat16),
             pltpu.VMEM((rows, model_width), jnp.bfloat16),
@@ -339,7 +345,7 @@
         compiler_params=pltpu.CompilerParams(
             collective_id=0, has_side_effects=True, vmem_limit_bytes=60 * 1024 * 1024
         ),
-    )(embeddings, weights, label_lanes)
+    )(embeddings, weights, labels.reshape(slabs, LANES))
     tall = model_width // 2
     update = pl.pallas_call(
         functools.partial(update_kernel, rate),
@@ -351,10 +357,10 @@
         ],
         out_specs=pl.BlockSpec((tall, width), lambda c, i: (i, c)),
         compiler_params=pltpu.CompilerParams(
-            dimension_semantics=("arbitrary", "arbitrary"), vmem_limit_bytes=32 * 1024 * 1024
+            dimension_semantics=("arbitrary", "arbitrary"), vmem_limit_bytes=60 * 1024 * 1024
         ),
     )(turned, total)
-    return update, losses.reshape(STEPS, rows)
+    return update, losses
 
 
 def shards(embeddings, weights, labels):

time: 180 us -> 175 us (0.972)
  local copies, waits for them, and re-layouts: 6.37 us -> 0.6 us
  Pallas kernels: 172 us -> 174 us
    pallas_call x1, Pallas kernels: 9.11 us -> 16.1 us  [fused(): pl.pallas_call(functools.partial(update_kernel, rate), grid=(chunks, 2),...]
    pallas_call x1, Pallas kernels: 163 us -> 158 us  [fused(): pl.pallas_call(functools.partial(exchange_kernel, cls_n, row_n, rate), ou...]
    unnamed x5 -> x3, local copies, waits for them, and re-layouts: 5.38 us -> 0.6 us
where the time goes in v3:
time: 175 us
  Pallas kernels  174 us (99%)
    pallas_call x1, Pallas kernels, fused(): pl.pallas_call(functools.partial(exchange_kernel, cls_n, row_n, rate), ou...  158 us
    pallas_call x1, Pallas kernels, fused(): pl.pallas_call(functools.partial(update_kernel, rate), grid=(chunks, 2),...  16.1 us

profile of v3, /device:TPU:0, one launch (start us, length us, event | category | flops | bytes accessed | tf_op | source)
XLA Modules:
  0.0 175.1 jit_solution(15722346554042825376)
XLA Ops:
  0.6 157.8 %shard_map.50 = (bf16[5,1024,512]{2,1,0:T(8,128)(2,1)}, bf16[1024,1024]{1,0:T(8,128)(2,1)}, f32[2,1024]{1,0:T(2,128)}) custom-call(f32[256,1024]{1,0:T(8,128)} %emb_ref.1, f32[32,81920]{1,0:T(8,128)} %weights_ref.1, s32[8,128]{1,0:T(8,128)} %bitcast.1), custom_call_target="tpu_custom_call" | custom-call | tf_op jit(solution)/shard_map/pallas_call | solution.py:309
  158.4 0.0 copy-start
  158.4 16.1 %shard_map.51 = f32[1024,2560]{1,0:T(8,128)} custom-call(bf16[1024,1024]{1,0:T(8,128)(2,1)} %get-tuple-element.5.turned_ref, bf16[5,1024,512]{2,1,0:T(8,128)(2,1)} %get-tuple-element.6.total_ref), custom_call_target="tpu_custom_call" | custom-call | tf_op jit(solution)/shard_map/pallas_call | solution.py:350
  174.5 0.0 copy-done
  174.5 0.6 copy.6
Async XLA Ops:
  158.4 16.1 %copy-start = (f32[2,1024]{1,0:T(2,128)S(1)}, f32[2,1024]{1,0:T(2,128)}, u32[]{:S(2)}) copy-start(f32[2,1024]{1,0:T(2,128)} %get-tuple-element.11) | copy-start | bytes 24580
